TPU v7x, 256 devices: a 2x2x32 block of a 4x8x32 slice. The times are simulated.
256 devices in a mesh: groups: 4 (over y, x), az: 64 (over z, core).
Axes of the slice: x: 2, y: 2, z: 32, core: 2. Of those that a mesh axis runs over, the one named last changes fastest.
The devices are a block of a 4x8x32 slice.
Arguments:
- sweep_stack: bfloat16 [2, 4, 256, 80, 2560], P(None, None, ('groups', 'az')), parts along dimension 2
- blend_curve: bfloat16 [256, 80], P(('groups', 'az')), parts along dimension 0, may hold values from 0.25 to 4
- sweep_start_index: int32 [256], P(('groups', 'az')), parts along dimension 0, may hold values from -20 to 2530, as said below
- usable_azimuth_extent: int32 [256, 2], P(('groups', 'az')), parts along dimension 0, may hold values from 0 to 80, as said below
- usable_column_extent: int32 [256, 2], P(('groups', 'az')), parts along dimension 0, may hold values from 0 to 2560, as said below
- image_couples: int32 [16, 2], P('groups'), parts along dimension 0, may hold values from 0 to 3, as said below
Outputs:
- interferogram: float32 [2, 16, 512, 128], P(None, 'groups', 'az'), parts along dimension 1
- coherence: float32 [16, 512, 128], P('groups', 'az'), parts along dimension 0
There are 4 independent parts, one for each index of `groups`. A program takes and returns all parts, laid end to end along the dimension named above; each array names one. Nothing has to cross between parts.
Inputs may be any that keep to these rules, and one draw needn't show every extreme that they name: `sweep_start_index`: the valid lines of burst b lie at merged rows from b * 40 - 15 to (b + 1) * 40 + 14, and some burst reaches both ends. The valid lines of all bursts together cover every merged row from 0 to 2559. `usable_azimuth_extent`: first below end for every burst. `usable_column_extent`: first below end for every burst. `image_couples`: the two acquisitions of a pair differ.
All inputs are finite; a program needn't handle non-finite values.
Results may differ from a plain program's by a relative error of at most 0.0003.
Values may be sent and summed in bfloat16 or wider, within the bound.
A program may use at most 64 MiB of HBM per device.

v0:
```python
import jax
import jax.numpy as jnp
from jax import lax
from jax.sharding import PartitionSpec as P

BLOCK_HEIGHT = 40
SLANT_WIDTH = 2560
LOOK_ROWS = 5
LOOK_COLS = 20
MARGIN = 15
SWEEP_HEIGHT = 80


def from_behind(block, axis, distance):
    devices = range(lax.axis_size(axis))
    route = [(i - distance, i) for i in devices if i - distance in devices]
    return lax.ppermute(block, axis, route)


def looked(values, column_box):
    shaped = values.reshape(
        values.shape[:-2] + (values.shape[-2] // LOOK_ROWS, LOOK_ROWS, values.shape[-1])
    )
    aggregate = jnp.sum(shaped, axis=-2)
    return jnp.dot(aggregate, column_box, precision=lax.Precision.HIGHEST)


def weighted(raw_lines, weights):
    return raw_lines.astype(jnp.float32) * weights.astype(jnp.float32)[:, None]


def per_device(
    sweep_stack,
    blend_curve,
    sweep_start_index,
    usable_azimuth_extent,
    usable_column_extent,
    image_couples,
):
    sweep_content = sweep_stack[:, :, 0]
    block_height = BLOCK_HEIGHT
    azimuth_index = jnp.arange(SWEEP_HEIGHT, dtype=jnp.int32)
    column_index = jnp.arange(SLANT_WIDTH, dtype=jnp.int32)
    line_valid = (azimuth_index >= usable_azimuth_extent[0, 0]) & (
        azimuth_index < usable_azimuth_extent[0, 1]
    )
    azimuth_blend = jnp.where(line_valid, blend_curve[0], jnp.zeros((), jnp.bfloat16))
    sample_valid = (column_index >= usable_column_extent[0, 0]) & (
        column_index < usable_column_extent[0, 1]
    )
    index_shift = sweep_start_index[0] - (lax.axis_index("az") - 1) * block_height

    def gather_lines(start_index, count):
        desired = start_index + jnp.arange(count, dtype=jnp.int32) - index_shift
        within_extent = (desired >= 0) & (desired < SWEEP_HEIGHT)
        bounded_indices = jnp.clip(desired, 0, SWEEP_HEIGHT - 1)
        chosen_indices = jnp.take(sweep_content, bounded_indices, axis=2)
        raw_lines = jnp.where(sample_valid, chosen_indices, jnp.zeros((), jnp.bfloat16))
        matches = bounded_indices[:, None] == azimuth_index[None, :]
        weights = jnp.sum(
            jnp.where(matches, azimuth_blend[None, :], jnp.zeros((), jnp.bfloat16)), axis=1
        )
        weights = jnp.where(within_extent, weights, jnp.zeros((), jnp.bfloat16))
        return (raw_lines, weights)

    extent_rows = MARGIN
    middle_lines, middle_weights = gather_lines(block_height, block_height)
    lower_lines, lower_weights = gather_lines(block_height - extent_rows, extent_rows)
    upper_lines, upper_weights = gather_lines(2 * block_height, extent_rows)
    above_lines, above_weights = from_behind((lower_lines, lower_weights), "az", -1)
    below_lines, below_weights = from_behind((upper_lines, upper_weights), "az", 1)
    from_above = weighted(above_lines, above_weights)
    from_below = weighted(below_lines, below_weights)
    cross_term = weighted(middle_lines, middle_weights)
    cross_term = cross_term.at[:, :, block_height - extent_rows :].add(from_above)
    cross_term = cross_term.at[:, :, :extent_rows].add(from_below)
    intensity_norm = middle_weights.astype(jnp.float32)
    intensity_norm = intensity_norm.at[block_height - extent_rows :].add(
        above_weights.astype(jnp.float32)
    )
    intensity_norm = intensity_norm.at[:extent_rows].add(below_weights.astype(jnp.float32))
    combined_grid = cross_term / intensity_norm[:, None]
    intensity = combined_grid[0] * combined_grid[0] + combined_grid[1] * combined_grid[1]
    first_image = jnp.take(combined_grid, image_couples[:, 0], axis=1)
    second_image = jnp.take(combined_grid, image_couples[:, 1], axis=1)
    real_part = first_image[0] * second_image[0] + first_image[1] * second_image[1]
    imag_part = first_image[1] * second_image[0] - first_image[0] * second_image[1]
    column_box = (
        column_index[:, None] // LOOK_COLS
        == jnp.arange(SLANT_WIDTH // LOOK_COLS, dtype=jnp.int32)[None, :]
    ).astype(jnp.float32)
    look_sum = looked(jnp.stack([real_part, imag_part]), column_box)
    look_power = looked(intensity, column_box)
    power_first = jnp.take(look_power, image_couples[:, 0], axis=0)
    power_second = jnp.take(look_power, image_couples[:, 1], axis=0)
    coherence = (look_sum[0] * look_sum[0] + look_sum[1] * look_sum[1]) / jnp.maximum(
        power_first * power_second, 1.0
    )
    interferogram = look_sum / (LOOK_ROWS * LOOK_COLS)
    return (interferogram, coherence)


def solution(mesh):
    return jax.shard_map(
        per_device,
        mesh=mesh,
        in_specs=(
            P(None, None, ("groups", "az"), None, None),
            P(("groups", "az"), None),
            P(("groups", "az")),
            P(("groups", "az"), None),
            P(("groups", "az"), None),
            P("groups", None),
        ),
        out_specs=(P(None, "groups", "az", None), P("groups", "az", None)),
        check_vma=False,
    )
```

profile of v0, /device:TPU:37, one launch (start us, length us, event | category | flops | bytes accessed | tf_op | source)
XLA Modules:
  0.0 83.8 jit_solution(6345981178381013266)
XLA Ops:
  1.3 1.4 %fusion.33 = (s32[1,1]{1,0:T(1,128)}, s32[1,1]{1,0:T(1,128)}) fusion(s32[1,2]{1,0:T(1,128)} %param.23), kind=kLoop, calls=%fused_computation.92 | loop fusion | bytes 16 | tf_op jit(solution)/shard_map/slice | solution.py:44
  2.7 1.9 %fusion.27 = bf16[80]{0:T(256)(128)(2,1)S(1)} fusion(bf16[1,80]{1,0:T(2,128)(2,1)} %param.21, s32[]{:T(128)} %bitcast.7, s32[]{:T(128)} %bitcast.6), kind=kLoop, calls=%fused_computation.85 | loop fusion | flops 320 | bytes 328 | tf_op jit(solution)/shard_map/jit(_where)/broadcast_in_dim | solution.py:61
  4.6 0.2 fusion.24
  4.8 22.4 %collective-permute-start.1 = (bf16[15]{0:T(256)(128)(2,1)S(1)}, bf16[15]{0:T(256)(128)(2,1)S(1)}, u32[]{:S(2)}, u32[]{:S(2)}) collective-permute-start(bf16[15]{0:T(256)(128)(2,1)S(1)} %and_select_fusion.1), channel_id=1, source_target_pairs={{1,0},{2,1},{3,2},{4,3},{5,4},{6,5},{7,6},{8,7},{9,8},{10,9},{11,1... | collective-permute-start | bytes 98 | tf_op jit(solution)/shard_map/ppermute | solution.py:17
  27.2 2.0 %collective-permute-start.3 = (bf16[15]{0:T(256)(128)(2,1)S(1)}, bf16[15]{0:T(256)(128)(2,1)S(1)}, u32[]{:S(2)}, u32[]{:S(2)}) collective-permute-start(bf16[15]{0:T(256)(128)(2,1)S(1)} %and_select_fusion), channel_id=1, source_target_pairs={{0,1},{1,2},{2,3},{3,4},{4,5},{5,6},{6,7},{7,8},{8,9},{9,10},{10,1... | collective-permute-start | bytes 98 | tf_op jit(solution)/shard_map/ppermute | solution.py:17
  29.2 1.3 %fusion.32 = (s32[1,1]{1,0:T(1,128)}, s32[1,1]{1,0:T(1,128)}) fusion(s32[1,2]{1,0:T(1,128)} %param.24), kind=kLoop, calls=%fused_computation.91 | loop fusion | bytes 16 | tf_op jit(solution)/shard_map/slice | solution.py:48
  30.5 4.5 %copy.51 = bf16[2,4,1,80,2560]{4,1,3,0,2:T(4,128)(2,1)S(1)} copy(bf16[2,4,1,80,2560]{4,3,2,1,0:T(8,128)(2,1)} %param.20) | data formatting | bytes 6553600 | tf_op args[0]
  35.0 1.9 %gather_fusion.2 = bf16[15,2,4,2560]{3,2,1,0:T(4,128)(2,1)} fusion(bf16[2,4,80,2560]{3,1,2,0:T(4,128)(2,1)S(1)} %bitcast.48, s32[1024]{0:T(1024)S(1)} %pad_clamp_fusion.2), kind=kCustom, calls=%fused_computation.3.clone | custom fusion | bytes 1228860 | tf_op jit(solution)/shard_map/jit(_take)/gather | solution.py:57
  36.8 0.0 copy-start.1
  36.8 1.9 %gather_fusion.1 = bf16[15,2,4,2560]{3,2,1,0:T(4,128)(2,1)} fusion(bf16[2,4,80,2560]{3,1,2,0:T(4,128)(2,1)S(1)} %bitcast.49, s32[1024]{0:T(1024)S(1)} %pad_clamp_fusion.3), kind=kCustom, calls=%fused_computation.clone | custom fusion | bytes 1228860 | tf_op jit(solution)/shard_map/jit(_take)/gather | solution.py:57
  38.7 1.3 %fusion.19 = pred[2560]{0:T(1024)(128)(4,1)S(1)} fusion(s32[]{:T(128)} %bitcast.2, s32[]{:T(128)} %bitcast.1), kind=kLoop, calls=%fused_computation.51 | loop fusion | flops 7680 | bytes 2568 | tf_op jit(solution)/shard_map/and | solution.py:48
  40.0 3.0 %bitcast_select_fusion = (bf16[2,4,15,2560]{3,1,0,2:T(4,128)(2,1)}, bf16[2,4,15,2560]{3,1,0,2:T(4,128)(2,1)}) fusion(bf16[15,2,4,2560]{3,2,1,0:T(4,128)(2,1)} %gather_fusion.2, pred[15]{0:T(512)(128)(4,1)S(1)} %get-tuple-element.77, pred[2560]{0:T(1024)(128)(4,1)S(1)} %fusion.19, bf16[15,2,4,2560]{3,2,1,0:T(4,128)(2,1)} %gather_fusion.1, ...), kind=kLoop, calls=%fused_computation.29 | loop fusion | flops 1228800 | bytes 2460190 | tf_op jit(solution)/shard_map/jit(_where)/select_n | solution.py:58
  43.0 1.9 %collective-permute-start.2 = (bf16[2,4,15,2560]{3,1,0,2:T(4,128)(2,1)}, bf16[2,4,15,2560]{3,1,0,2:T(4,128)(2,1)}, u32[]{:S(2)}, u32[]{:S(2)}) collective-permute-start(bf16[2,4,15,2560]{3,1,0,2:T(4,128)(2,1)} %get-tuple-element.65), channel_id=1, source_target_pairs={{0,1},{1,2},{2,3},{3,4},{4,5},{5,6},{6,7},{7,8},{8,9},{9,10},{10,1... | collective-permute-start | bytes 1843208 | tf_op jit(solution)/shard_map/ppermute | solution.py:17
  45.0 3.4 %collective-permute-start = (bf16[2,4,15,2560]{3,1,0,2:T(4,128)(2,1)}, bf16[2,4,15,2560]{3,1,0,2:T(4,128)(2,1)}, u32[]{:S(2)}, u32[]{:S(2)}) collective-permute-start(bf16[2,4,15,2560]{3,1,0,2:T(4,128)(2,1)} %get-tuple-element.66), channel_id=1, source_target_pairs={{1,0},{2,1},{3,2},{4,3},{5,4},{6,5},{7,6},{8,7},{9,8},{10,9},{11,1... | collective-permute-start | bytes 1843208 | tf_op jit(solution)/shard_map/ppermute | solution.py:17
  48.4 0.2 fusion.21
  48.6 0.0 copy-done.1
  48.7 3.4 %gather_fusion = bf16[40,2,4,2560]{3,2,1,0:T(4,128)(2,1)} fusion(bf16[2,4,80,2560]{3,1,2,0:T(4,128)(2,1)S(1)} %bitcast.50, s32[1024]{0:T(1024)S(1)} %pad_clamp_fusion.4), kind=kCustom, calls=%fused_computation.6 | custom fusion | bytes 3276960 | tf_op jit(solution)/shard_map/jit(_take)/gather | solution.py:57
  52.1 2.6 %multiply_bitcast_fusion = f32[2,4,40,2560]{3,1,0,2:T(4,128)S(1)} fusion(f32[40]{0:T(128)S(1)} %fusion.28, bf16[40,2,4,2560]{3,2,1,0:T(4,128)(2,1)} %gather_fusion, pred[40]{0:T(512)(128)(4,1)S(1)} %compare_and_fusion.4, pred[2560]{0:T(1024)(128)(4,1)S(1)} %fusion.19), kind=kLoop, calls=%fused_computation.11 | loop fusion | flops 3276800 | bytes 4917960 | tf_op jit(solution)/shard_map/mul | solution.py:29
  54.7 0.0 collective-permute-done.1
  54.7 0.0 collective-permute-done.3
  54.7 0.1 add_dynamic-update-slice_fusion
  54.9 1.9 %collective-permute-done = bf16[2,4,15,2560]{3,1,0,2:T(4,128)(2,1)} collective-permute-done((bf16[2,4,15,2560]{3,1,0,2:T(4,128)(2,1)}, bf16[2,4,15,2560]{3,1,0,2:T(4,128)(2,1)}, u32[]{:S(2)}, u32[]{:S(2)}) %collective-permute-start) | collective-permute-done | bytes 614432 | tf_op jit(solution)/shard_map/ppermute | solution.py:17
  56.8 1.6 %fusion.8 = f32[2,4,40,2560]{3,1,0,2:T(4,128)S(1)} fusion(f32[2,4,40,2560]{3,1,0,2:T(4,128)S(1)} %multiply_bitcast_fusion, bf16[2,4,15,2560]{3,1,0,2:T(4,128)(2,1)} %collective-permute-done, f32[15]{0:T(128)S(1)} %convert_element_type.35), kind=kLoop, calls=%fused_computation.26 | loop fusion | flops 921600 | bytes 3072512 | tf_op jit(solution)/shard_map/scatter-add | solution.py:75
  58.4 0.0 collective-permute-done.2
  58.4 1.6 %fusion.7 = f32[2,4,40,2560]{3,1,0,2:T(4,128)S(1)} fusion(f32[2,4,40,2560]{3,1,0,2:T(4,128)S(1)} %fusion.8, bf16[2,4,15,2560]{3,1,0,2:T(4,128)(2,1)} %collective-permute-done.2, f32[15]{0:T(128)S(1)} %convert_element_type.37), kind=kLoop, calls=%fused_computation.24 | loop fusion | flops 921600 | bytes 3072512 | tf_op jit(solution)/shard_map/scatter-add | solution.py:76
  60.1 0.9 %broadcast_divide_fusion = f32[2,4,40,2560]{3,1,0,2:T(4,128)S(1)} fusion(f32[2,4,40,2560]{3,1,0,2:T(4,128)S(1)} %fusion.7, f32[40]{0:T(128)S(1)} %constant_dynamic-update-slice_fusion), kind=kLoop, calls=%fused_computation.17 | loop fusion | flops 819200 | bytes 6553760 | tf_op jit(solution)/shard_map/div | solution.py:82
  61.0 1.6 %fusion = f32[1,4,40,2560]{3,1,0,2:T(4,128)} fusion(f32[2,4,40,2560]{3,1,0,2:T(4,128)S(1)} %broadcast_divide_fusion), kind=kLoop, calls=%fused_computation.13 | loop fusion | flops 1228800 | bytes 4915200 | tf_op jit(solution)/shard_map/add | solution.py:83
  62.6 1.9 %copy.29 = f32[2,4,40,2560]{3,2,1,0:T(8,128)S(1)} copy(f32[2,4,40,2560]{3,1,0,2:T(4,128)S(1)} %broadcast_divide_fusion) | data formatting | bytes 6553600 | tf_op jit(solution)/shard_map/div | solution.py:82
  64.5 2.5 %reduce_sum.58 = f32[4,8,2560]{2,0,1:T(4,128)} reduce(f32[4,8,5,2560]{3,0,2,1:T(4,128)} %bitcast.52, f32[]{:T(128)} %constant.178.clone.1), dimensions={2}, to_apply=%region_4.7 | reduce | flops 327680 | bytes 1966084 | tf_op jit(solution)/shard_map/reduce_sum | solution.py:24
  67.0 1.8 %fusion.5 = f32[4,8,128]{2,0,1:T(4,128)S(1)} fusion(f32[4,8,2560]{2,0,1:T(4,128)} %reduce_sum.58, s32[2560]{0:T(1024)S(1)} %add_select_fusion), kind=kOutput, calls=%fused_computation.22 | convolution fusion | flops 126156800 | bytes 354304 | tf_op jit(solution)/shard_map/dot_general | solution.py:25
  68.8 0.6 gather_fusion.6
  69.3 0.6 gather_fusion.5
  69.9 2.4 %gather_fusion.3 = f32[4,2,40,2560]{3,2,1,0:T(8,128)} fusion(f32[2,4,40,2560]{3,2,1,0:T(8,128)S(1)} %copy.29, s32[1024]{0:T(1024)S(1)} %get-tuple-element.82), kind=kCustom, calls=%fused_computation.1.clone | custom fusion | bytes 6553616 | tf_op jit(solution)/shard_map/jit(_take)/gather | solution.py:84
  72.3 2.5 %gather_fusion.4 = f32[4,2,40,2560]{3,2,1,0:T(8,128)} fusion(f32[2,4,40,2560]{3,2,1,0:T(8,128)S(1)} %copy.29, s32[1024]{0:T(1024)S(1)} %get-tuple-element.81), kind=kCustom, calls=%fused_computation.4.clone | custom fusion | bytes 6553616 | tf_op jit(solution)/shard_map/jit(_take)/gather | solution.py:85
  74.8 0.0 copy-start
  74.8 2.5 %select_bitcast_fusion = f32[2,4,40,2560]{3,2,0,1:T(8,128)S(1)} fusion(f32[4,2,40,2560]{3,2,1,0:T(8,128)} %gather_fusion.4, pred[4]{0:T(512)(128)(4,1)S(1)} %get-tuple-element.67), kind=kLoop, calls=%fused_computation.9 | loop fusion | flops 819200 | bytes 6553604 | tf_op jit(solution)/shard_map/jit(_take)/select_n | solution.py:85
  77.3 0.4 copy-done
  77.7 0.4 select_bitcast_fusion.1
  78.1 0.6 multiply_add_fusion
  78.7 1.1 %copy.31 = f32[1,4,40,2560]{3,1,2,0:T(4,128)S(1)} copy(f32[1,4,40,2560]{3,2,0,1:T(8,128)S(1)} %get-tuple-element.63) | data formatting | bytes 3276800 | tf_op jit(solution)/shard_map/add | solution.py:86
  79.7 1.1 %copy.32 = f32[1,4,40,2560]{3,1,2,0:T(4,128)S(1)} copy(f32[1,4,40,2560]{3,2,0,1:T(8,128)S(1)} %get-tuple-element.64) | data formatting | bytes 3276800 | tf_op jit(solution)/shard_map/sub | solution.py:87
  80.8 0.8 maximum_reduce_fusion
  81.6 0.9 %broadcast_multiply_fusion = (f32[2,4,8,128]{3,1,2,0:T(4,128)S(1)}, f32[2,4,8,128]{3,1,2,0:T(4,128)S(1)}) fusion(f32[2,4,8,2560]{3,1,2,0:T(4,128)S(1)} %maximum_reduce_fusion, s32[2560]{0:T(1024)S(1)} %add_select_fusion), kind=kOutput, calls=%fused_computation.46 | convolution fusion | flops 251994112 | bytes 731136 | tf_op jit(solution)/shard_map/dot_general | solution.py:25
  82.5 0.6 copy.37
  83.1 0.1 fusion.14
  83.2 0.6 copy.38
  (19 shorter events, 0.2 us)
Async XLA Ops:
  4.8 49.9 %collective-permute-start.1 = (bf16[15]{0:T(256)(128)(2,1)S(1)}, bf16[15]{0:T(256)(128)(2,1)S(1)}, u32[]{:S(2)}, u32[]{:S(2)}) collective-permute-start(bf16[15]{0:T(256)(128)(2,1)S(1)} %and_select_fusion.1), channel_id=1, source_target_pairs={{1,0},{2,1},{3,2},{4,3},{5,4},{6,5},{7,6},{8,7},{9,8},{10,9},{11,1... | collective-permute-start | bytes 98 | tf_op jit(solution)/shard_map/ppermute | solution.py:17
  27.2 27.6 %collective-permute-start.3 = (bf16[15]{0:T(256)(128)(2,1)S(1)}, bf16[15]{0:T(256)(128)(2,1)S(1)}, u32[]{:S(2)}, u32[]{:S(2)}) collective-permute-start(bf16[15]{0:T(256)(128)(2,1)S(1)} %and_select_fusion), channel_id=1, source_target_pairs={{0,1},{1,2},{2,3},{3,4},{4,5},{5,6},{6,7},{7,8},{8,9},{9,10},{10,1... | collective-permute-start | bytes 98 | tf_op jit(solution)/shard_map/ppermute | solution.py:17
  36.8 11.8 %copy-start.1 = (s32[4,2]{0,1:T(2,128)S(1)}, s32[4,2]{0,1:T(2,128)}, u32[]{:S(2)}) copy-start(s32[4,2]{0,1:T(2,128)} %param.25) | copy-start | bytes 100
  43.0 15.4 %collective-permute-start.2 = (bf16[2,4,15,2560]{3,1,0,2:T(4,128)(2,1)}, bf16[2,4,15,2560]{3,1,0,2:T(4,128)(2,1)}, u32[]{:S(2)}, u32[]{:S(2)}) collective-permute-start(bf16[2,4,15,2560]{3,1,0,2:T(4,128)(2,1)} %get-tuple-element.65), channel_id=1, source_target_pairs={{0,1},{1,2},{2,3},{3,4},{4,5},{5,6},{6,7},{7,8},{8,9},{9,10},{10,1... | collective-permute-start | bytes 1843208 | tf_op jit(solution)/shard_map/ppermute | solution.py:17
  45.0 11.8 %collective-permute-start = (bf16[2,4,15,2560]{3,1,0,2:T(4,128)(2,1)}, bf16[2,4,15,2560]{3,1,0,2:T(4,128)(2,1)}, u32[]{:S(2)}, u32[]{:S(2)}) collective-permute-start(bf16[2,4,15,2560]{3,1,0,2:T(4,128)(2,1)} %get-tuple-element.66), channel_id=1, source_target_pairs={{1,0},{2,1},{3,2},{4,3},{5,4},{6,5},{7,6},{8,7},{9,8},{10,9},{11,1... | collective-permute-start | bytes 1843208 | tf_op jit(solution)/shard_map/ppermute | solution.py:17
  74.8 2.9 %copy-start = (f32[4,2,40,2560]{3,2,1,0:T(8,128)S(1)}, f32[4,2,40,2560]{3,2,1,0:T(8,128)}, u32[]{:S(2)}) copy-start(f32[4,2,40,2560]{3,2,1,0:T(8,128)} %gather_fusion.3) | copy-start | bytes 9830404
where the time goes:
time: 84.3 us; the launch traced here: 83.8 us
  starting transfers between devices  29.7 us (35%)
  local copies, waits for them, and re-layouts  25.9 us (31%)
  other arithmetic  22.1 us (26%)
  matrix products  2.61 us (3%)
  waiting for transfers between devices  1.88 us (2%)
  between operations  1.55 us (2%)
    ppermute x4, starting transfers between devices, from_behind(): return lax.ppermute(block, axis, route)  29.7 us
    gather x3, local copies, waits for them, and re-layouts, gather_lines(): chosen_indices = jnp.take(sweep_content, bounded_indices, axis=2)  7.13 us
    unnamed x7, local copies, waits for them, and re-layouts  6.1 us
    reduce_sum x2, other arithmetic, looked(): aggregate = jnp.sum(shaped, axis=-2)  3.3 us
    select_n x1, other arithmetic, gather_lines(): jnp.where(sample_valid, chosen_indices, jnp.zeros((), jnp.bfloat16))  3.01 us
    mul x1, other arithmetic, weighted(): return raw_lines.astype(jnp.float32) * weights.astype(jnp.float32)[:, None]  2.61 us
    dot_general x2, matrix products, looked(): return jnp.dot(aggregate, column_box, precision=lax.Precision.HIGHEST)  2.61 us
    select_n x1, other arithmetic, per_device(): second_image = jnp.take(combined_grid, image_couples[:, 1], axis=1)  2.49 us
  transfers between devices with their start and end apart: 4, of which 1 were waited for; matrix products, arithmetic and copies ran while one was open for 26% of the time, Pallas kernels for 0%

commit v1 on v0

v1 whole, which is shorter than its diff:
```python
import functools

import jax
import jax.numpy as jnp
from jax import lax
from jax.experimental import pallas as pl
from jax.experimental.pallas import tpu as pltpu
from jax.sharding import PartitionSpec as P

BLOCK_HEIGHT = 40
LOOK_ROWS = 5
LOOK_COLS = 20
MARGIN = 15
LANES = 256
CHUNK = 2 * LANES
SUB = 16
F32, BF16, I32 = jnp.float32, jnp.bfloat16, jnp.int32


def iota(shape, dimension):
    return lax.broadcasted_iota(I32, shape, dimension)


def own_row(position):
    looks = BLOCK_HEIGHT // LOOK_ROWS
    return LOOK_ROWS * (position % looks) + position // looks


def kernel(
    ring,
    x_hbm,
    blend_hbm,
    start_hbm,
    lines_hbm,
    columns_hbm,
    couples_hbm,
    ifg_ref,
    coh_ref,
    x,
    stage,
    recv,
    own,
    spread,
    boxes,
    total,
    note,
    heard,
    blend,
    start,
    lines,
    columns,
    couples,
    x_sem,
    small_sem,
    send_sem,
    recv_sem,
    note_send,
    note_recv,
):
    chunks, planes, height, _ = x.shape
    images = planes // 2
    duos = [(i, j) for i in range(images) for j in range(i + 1, images)]
    pairs = couples.shape[1]
    looks = BLOCK_HEIGHT // LOOK_ROWS
    me = lax.axis_index("az")
    above, below = lax.rem(me + ring - 1, ring), lax.rem(me + 1, ring)
    targets = (above, below)

    small = [
        pltpu.make_async_copy(source, target, small_sem.at[i])
        for i, (source, target) in enumerate(
            (
                (blend_hbm, blend),
                (start_hbm, start),
                (lines_hbm, lines),
                (columns_hbm, columns),
                (couples_hbm, couples),
            )
        )
    ]
    for copy in small:
        copy.start()
    loads = [
        pltpu.make_async_copy(
            x_hbm.at[:, :, pl.ds(c * CHUNK, CHUNK)], x.at[c], x_sem.at[c]
        )
        for c in range(chunks)
    ]
    for copy in loads:
        copy.start()

    barrier = pltpu.get_barrier_semaphore()
    for target in targets:
        pl.semaphore_signal(
            barrier, inc=1, device_id={"az": target}, device_id_type=pl.DeviceIdType.MESH
        )

    for copy in small:
        copy.wait()
    shift = start[0, 0] - me * BLOCK_HEIGHT
    line = iota((1, height), 1)
    valid = (line >= lines[0, 0]) & (line < lines[0, 1])
    weight = jnp.where(valid, blend[...].astype(F32), 0.0)

    far = planes - 1
    absent = -1000
    bases = (-MARGIN, BLOCK_HEIGHT)

    def own_target(rows, first):
        return own_row(iota((rows, 1), 0) - first)

    def selection(rows, target, first_own):
        row = iota((rows, 1), 0)
        matches = (iota((rows, height), 1) + shift) == target
        values = jnp.where(row < first_own, 1.0, weight)
        return jnp.where(matches, values, 0.0)

    row = iota((2 * SUB + BLOCK_HEIGHT, 1), 0)
    tile_row = row % SUB
    target = jnp.where(row < SUB, bases[0], bases[1]) + tile_row
    target = jnp.where(tile_row == MARGIN, absent, target)
    target = jnp.where(row >= 2 * SUB, own_target(row.shape[0], 2 * SUB), target)
    select_near_f32 = selection(row.shape[0], target, 2 * SUB)
    select_near = select_near_f32.astype(BF16)
    rest = SUB // 2
    groups = rest * far
    far_own = 2 * rest + 2 * groups
    row = iota((far_own + BLOCK_HEIGHT, 1), 0)
    sub = row % rest
    up_side = (row < rest) | ((row >= 2 * rest) & (row < 2 * rest + groups))
    member = jnp.where(up_side, row - 2 * rest, row - 2 * rest - groups) // rest
    offset = jnp.where(row < 2 * rest, far + sub, jnp.where(sub == rest - 1, member, absent))
    target = jnp.where(up_side, bases[0], bases[1]) + offset
    target = jnp.where(row >= far_own, own_target(row.shape[0], far_own), target)
    select_far = selection(row.shape[0], target, far_own).astype(BF16)

    lane = iota((1, LANES), 1)
    side, place = lane // (LANES // 2), lane % (LANES // 2)
    tile, inner = place // SUB, place % SUB

    def origin(half):
        tail = inner - rest * half
        in_tail = tile == far
        kept = jnp.logical_not(in_tail) | ((tail >= 0) & (tail < rest))
        plane = jnp.where(in_tail | (inner == MARGIN), far, tile)
        offset = jnp.where(in_tail, far + tail, jnp.where(inner == MARGIN, tile, inner))
        return jnp.where(kept, plane, absent), offset

    eight = jnp.broadcast_to(weight, (8, height)).astype(BF16)
    for half in range(2):
        _, offset = origin(half)
        wanted = jnp.where(side == 0, bases[1], bases[0]) + offset
        picks = (iota((height, LANES), 0) + shift) == wanted
        sent = jnp.dot(
            eight, jnp.where(picks, 1.0, 0.0).astype(BF16), preferred_element_type=F32
        )
        note[1, pl.ds(8 * half, 8), :] = sent[:, : LANES // 2]
        note[0, pl.ds(8 * half, 8), :] = sent[:, LANES // 2 :]

    pl.semaphore_wait(barrier, 2)
    notes = [
        pltpu.make_async_remote_copy(
            src_ref=note.at[d],
            dst_ref=heard.at[1 - d],
            send_sem=note_send.at[d],
            recv_sem=note_recv.at[1 - d],
            device_id={"az": targets[d]},
            device_id_type=pl.DeviceIdType.MESH,
        )
        for d in range(2)
    ]

    def message(d, c):
        return pltpu.make_async_remote_copy(
            src_ref=stage.at[d, c],
            dst_ref=recv.at[1 - d, c],
            send_sem=send_sem.at[d, c],
            recv_sem=recv_sem.at[1 - d, c],
            device_id={"az": targets[d]},
            device_id_type=pl.DeviceIdType.MESH,
        )

    for copy in notes:
        copy.start()

    def outgoing(c, carry):
        pltpu.make_async_copy(
            x_hbm.at[:, :, pl.ds(pl.multiple_of(c * CHUNK, CHUNK), CHUNK)], x.at[c], x_sem.at[c]
        ).wait()
        column = iota((1, CHUNK), 1) + c * CHUNK
        seen = (column >= columns[0, 0]) & (column < columns[0, 1])
        mask = jnp.where(seen, 1.0, 0.0).astype(BF16)

        def product(matrix, p):
            return jnp.dot(matrix, x[c, p] * mask, preferred_element_type=F32)

        last = product(select_far, far)
        own[c, far] = last[far_own:]
        for d in range(2):
            tail = last[d * rest : (d + 1) * rest]
            stage[d, c, 2 * far] = jnp.concatenate(
                [tail[:, :LANES], tail[:, LANES:]], axis=0
            ).astype(BF16)
        for p in range(far):
            near = product(select_near, p)
            own[c, p] = near[2 * SUB :]
            for d in range(2):
                extra = 2 * rest + d * groups + rest * p
                block = jnp.concatenate(
                    [
                        near[d * SUB : d * SUB + rest],
                        near[d * SUB + rest : (d + 1) * SUB] + last[extra : extra + rest],
                    ],
                    axis=0,
                ).astype(BF16)
                stage[d, c, p] = block[:, :LANES]
                stage[d, c, far + p] = block[:, LANES:]
        for d in range(2):
            message(d, c).start()
        return carry

    lax.fori_loop(0, chunks, outgoing, 0)

    def box(c, carry):
        sample = iota((LANES, 128), 0) + c * LANES
        first = LOOK_COLS * iota((LANES, 128), 1)
        inside = (sample >= first) & (sample < first + LOOK_COLS)
        boxes[c] = jnp.where(inside, 1.0, 0.0).astype(BF16)
        return carry

    lax.fori_loop(0, 2 * chunks, box, 0)
    total[...] = jnp.zeros_like(total)

    for copy in notes:
        copy.wait()
    has = (
        jnp.where(me > 0, 1.0, 0.0).astype(F32),
        jnp.where(me < ring - 1, 1.0, 0.0).astype(F32),
    )
    norm = jnp.sum(select_near_f32[2 * SUB :], axis=1, keepdims=True)
    row_code = own_row(iota((BLOCK_HEIGHT, 1), 0))
    for half in range(2):
        plane, offset = origin(half)
        code = offset + jnp.where(side == 0, 0, BLOCK_HEIGHT - MARGIN)
        weights = jnp.concatenate(
            [heard[d, 8 * half : 8 * half + 1, :] * has[d] for d in range(2)], axis=1
        )
        for p in range(planes):
            matches = (row_code == code) & (plane == p)
            block = jnp.where(matches, weights, 0.0)
            spread[half, pl.ds(p * BLOCK_HEIGHT, BLOCK_HEIGHT), :] = block.astype(BF16)
            if half == 0 and p == 0:
                norm = norm + jnp.sum(block, axis=1, keepdims=True)
    scale = jnp.broadcast_to(1.0 / norm, (BLOCK_HEIGHT, LANES))

    def incoming(c, carry):
        for d in range(2):
            message(d, c).wait_recv()
        for half in range(2):
            tiles = []
            for d in range(2):
                tiles.append(recv[d, c, pl.ds(far * half, far)].reshape(far * SUB, LANES))
                tiles.append(recv[d, c, 2 * far])
            spill = jnp.dot(
                spread[half], jnp.concatenate(tiles, axis=0), preferred_element_type=F32
            )
            sums = [None] * (2 * len(duos) + images)

            def gather(slot, value):
                sums[slot] = value if sums[slot] is None else sums[slot] + value

            for within in range(LOOK_ROWS):
                rows = pl.ds(within * looks, looks)
                merged = []
                for p in range(planes):
                    at = p * BLOCK_HEIGHT + within * looks
                    merged.append(
                        (spill[at : at + looks] + own[c, p, rows, pl.ds(half * LANES, LANES)])
                        * scale[within * looks : (within + 1) * looks]
                    )
                re, im = merged[:images], merged[images:]
                for slot, (i, j) in enumerate(duos):
                    gather(slot, re[i] * re[j] + im[i] * im[j])
                    gather(len(duos) + slot, im[i] * re[j] - re[i] * im[j])
                for i in range(images):
                    gather(2 * len(duos) + i, re[i] * re[i] + im[i] * im[i])
            sums = jnp.concatenate(sums, axis=0)
            high = sums.astype(BF16)
            low = (sums - high.astype(F32)).astype(BF16)
            box_matrix = boxes[2 * c + half]
            total[...] += jnp.dot(high, box_matrix, preferred_element_type=F32) + jnp.dot(
                low, box_matrix, preferred_element_type=F32
            )
        return carry

    lax.fori_loop(0, chunks, incoming, 0)

    def looked(slot):
        return total[pl.ds(slot * looks, looks), :]

    def splat(value):
        return jnp.full((looks, total.shape[1]), value, I32)

    for p in range(pairs):
        i, j = splat(couples[0, p]), splat(couples[1, p])
        re = im = jnp.zeros(i.shape, F32)
        power_i = power_j = jnp.zeros(i.shape, F32)
        for slot, (a, b) in enumerate(duos):
            forward = (i == a) & (j == b)
            backward = (i == b) & (j == a)
            re = jnp.where(forward | backward, looked(slot), re)
            im = jnp.where(forward, looked(len(duos) + slot), im)
            im = jnp.where(backward, -looked(len(duos) + slot), im)
        for a in range(images):
            power_i = jnp.where(i == a, looked(2 * len(duos) + a), power_i)
            power_j = jnp.where(j == a, looked(2 * len(duos) + a), power_j)
        ifg_ref[0, p] = re / (LOOK_ROWS * LOOK_COLS)
        ifg_ref[1, p] = im / (LOOK_ROWS * LOOK_COLS)
        coh_ref[p] = (re * re + im * im) / jnp.maximum(power_i * power_j, 1.0)

    def drain(c, carry):
        for d in range(2):
            message(d, c).wait_send()
        return carry

    lax.fori_loop(0, chunks, drain, 0)


def per_device(ring, sweep_stack, blend, start, lines, columns, couples):
    parts, images, _, height, width = sweep_stack.shape
    planes = parts * images
    pairs = couples.shape[0]
    chunks = width // CHUNK
    looks = BLOCK_HEIGHT // LOOK_ROWS
    outputs = width // LOOK_COLS
    tiles = 2 * planes - 1
    hbm = pl.BlockSpec(memory_space=pltpu.HBM)
    vmem = pl.BlockSpec(memory_space=pltpu.VMEM)
    return pl.pallas_call(
        functools.partial(kernel, ring),
        name="merge",
        out_shape=(
            jax.ShapeDtypeStruct((parts, pairs, looks, outputs), F32),
            jax.ShapeDtypeStruct((pairs, looks, outputs), F32),
        ),
        in_specs=[hbm] * 6,
        out_specs=(vmem, vmem),
        scratch_shapes=[
            pltpu.VMEM((chunks, planes, height, CHUNK), BF16),
            pltpu.VMEM((2, chunks, tiles, SUB, LANES), BF16),
            pltpu.VMEM((2, chunks, tiles, SUB, LANES), BF16),
            pltpu.VMEM((chunks, planes, BLOCK_HEIGHT, CHUNK), F32),
            pltpu.VMEM((2, planes * BLOCK_HEIGHT, LANES), BF16),
            pltpu.VMEM((2 * chunks, LANES, outputs), BF16),
            pltpu.VMEM((images * images * looks, outputs), F32),
            pltpu.VMEM((2, 16, 128), F32),
            pltpu.VMEM((2, 16, 128), F32),
            pltpu.VMEM((1, height), BF16),
            pltpu.SMEM((1, 1), I32),
            pltpu.SMEM((1, 2), I32),
            pltpu.SMEM((1, 2), I32),
            pltpu.SMEM((2, pairs), I32),
            pltpu.SemaphoreType.DMA((chunks,)),
            pltpu.SemaphoreType.DMA((5,)),
            pltpu.SemaphoreType.DMA((2, chunks)),
            pltpu.SemaphoreType.DMA((2, chunks)),
            pltpu.SemaphoreType.DMA((2,)),
            pltpu.SemaphoreType.DMA((2,)),
        ],
        compiler_params=pltpu.CompilerParams(
            collective_id=0, has_side_effects=True
        ),
    )(
        sweep_stack.reshape(planes, height, width),
        blend,
        start.reshape(1, 1),
        lines,
        columns,
        couples.T,
    )


def solution(mesh):
    return jax.shard_map(
        functools.partial(per_device, mesh.shape["az"]),
        mesh=mesh,
        in_specs=(
            P(None, None, ("groups", "az"), None, None),
            P(("groups", "az"), None),
            P(("groups", "az")),
            P(("groups", "az"), None),
            P(("groups", "az"), None),
            P("groups", None),
        ),
        out_specs=(P(None, "groups", "az", None), P("groups", "az", None)),
        check_vma=False,
    )
```

time: 84.3 us -> 37.9 us (0.45)
  the two profiles are of different devices: /device:TPU:37 before, /device:TPU:46 now
where the time goes in v1:
time: 37.9 us; the launch traced here: 37.7 us
  Pallas kernels  33.7 us (89%)
  local copies, waits for them, and re-layouts  2.7 us (7%)
  between operations  1.28 us (3%)
    pallas_call x1, Pallas kernels, per_device(): pl.pallas_call(functools.partial(kernel, ring), name='merge', out_shape=(...  33.7 us
    unnamed x2, local copies, waits for them, and re-layouts  2.7 us

profile of v1, /device:TPU:46, one launch (start us, length us, event | category | flops | bytes accessed | tf_op | source)
XLA Modules:
  0.0 37.7 jit_solution(7377990327671886022)
XLA Ops:
  1.3 33.7 %merge.1 = (f32[2,4,8,128]{3,2,1,0:T(8,128)}, f32[4,8,128]{2,1,0:T(8,128)}) custom-call(bf16[8,80,2560]{2,1,0:T(8,128)(2,1)} %bitcast.4, bf16[1,80]{1,0:T(2,128)(2,1)} %blend_hbm.1, s32[1,1]{1,0:T(1,128)} %bitcast.3.start_hbm, s32[1,2]{1,0:T(1,128)} %lines_hbm.1, s32[1,2]{1,0:T(1,128)} %columns_hbm.1, s32[2,4]{1,0:T(2,128)} %bitcast.5), custom_call_target="tpu_custom_call" | custom-call | tf_op jit(solution)/shard_map/merge/pallas_call | solution.py:339
  35.0 1.4 %copy.11 = f32[2,4,8,128]{3,2,1,0:T(8,128)} copy(f32[2,4,8,128]{3,2,1,0:T(8,128)} %get-tuple-element.4) | data formatting | bytes 65536
  36.4 1.3 %copy.12 = f32[4,8,128]{2,1,0:T(8,128)} copy(f32[4,8,128]{2,1,0:T(8,128)} %get-tuple-element.5) | data formatting | bytes 32768

commit v2 on v0

v2 whole, which is shorter than its diff:
```python
import functools

import jax
import jax.numpy as jnp
from jax import lax
from jax.experimental import pallas as pl
from jax.experimental.pallas import tpu as pltpu
from jax.sharding import PartitionSpec as P

BLOCK_HEIGHT = 40
LOOK_ROWS = 5
LOOK_COLS = 20
MARGIN = 15
HALF = 256
CHUNK = 2 * HALF
SUB = 16
SIDES = 2
F32, BF16, I32 = jnp.float32, jnp.bfloat16, jnp.int32
MESH = pl.DeviceIdType.MESH


def iota(shape, dimension):
    return lax.broadcasted_iota(I32, shape, dimension)


def dot(a, b):
    return jnp.dot(a, b, preferred_element_type=F32)


def swap(block):
    half = block.shape[0] // 2
    return jnp.concatenate([block[half:], block[:half]], axis=0)


def merge(
    ring,
    x_hbm,
    blend_hbm,
    start_hbm,
    lines_hbm,
    columns_hbm,
    couples_hbm,
    ifg_ref,
    coh_ref,
    x,
    stage,
    recv,
    own,
    spread,
    boxes,
    spilled,
    split,
    total,
    note,
    heard,
    blend,
    start,
    lines,
    columns,
    couples,
    x_sem,
    small_sem,
    send_sem,
    recv_sem,
    note_send,
    note_recv,
    hello,
):
    chunks, planes, height, _ = x.shape
    images = planes // 2
    pairs = couples.shape[1]
    looks = BLOCK_HEIGHT // LOOK_ROWS
    quads = looks // SIDES
    duos = [(i, j) for i in range(images) for j in range(i + 1, images)]
    me = lax.axis_index("az")
    above, below = lax.rem(me + ring - 1, ring), lax.rem(me + 1, ring)
    targets = (above, below)
    present = (me > 0, me < ring - 1)

    small = [
        pltpu.make_async_copy(source, target, small_sem.at[i])
        for i, (source, target) in enumerate(
            (
                (start_hbm, start),
                (columns_hbm, columns),
                (lines_hbm, lines),
                (blend_hbm, blend),
                (couples_hbm, couples),
            )
        )
    ]

    def load(c):
        return pltpu.make_async_copy(
            x_hbm.at[:, :, pl.ds(c * CHUNK, CHUNK)], x.at[c], x_sem.at[c]
        )

    for copy in small[:3]:
        copy.start()
    load(0).start()
    for copy in small[3:]:
        copy.start()
    for c in range(1, chunks):
        load(c).start()

    barrier = pltpu.get_barrier_semaphore()

    @pl.when(present[0])
    def _():
        pl.semaphore_signal(barrier, inc=1, device_id={"az": above}, device_id_type=MESH)

    for side in range(SIDES):

        @pl.when(jnp.logical_not(present[side]))
        def _():
            heard[side] = jnp.zeros(heard.shape[1:], F32)
            for c in range(chunks):
                recv[side, c] = jnp.zeros(recv.shape[2:], BF16)

    def outgoing(side, c):
        return pltpu.make_async_remote_copy(
            src_ref=stage.at[side, c],
            dst_ref=recv.at[1 - side, c],
            send_sem=send_sem.at[side, c],
            recv_sem=recv_sem.at[1 - side, c],
            device_id={"az": targets[side]},
            device_id_type=MESH,
        )

    def words(side):
        return pltpu.make_async_remote_copy(
            src_ref=note.at[side],
            dst_ref=heard.at[1 - side],
            send_sem=note_send.at[side],
            recv_sem=note_recv.at[1 - side],
            device_id={"az": targets[side]},
            device_id_type=MESH,
        )

    for copy in small[:2]:
        copy.wait()
    shift = start[0, 0] - me * BLOCK_HEIGHT
    bases = (-MARGIN, BLOCK_HEIGHT)

    place = iota((1, 2 * height), 1)
    second = place >= height
    line = jnp.where(second, place - height, place)
    row_of_line = line + shift

    lead = iota((SIDES * 2 * SUB, 1), 0)
    inner = lead % SUB
    leaves = jnp.where(lead < 2 * SUB, bases[0], bases[1]) + inner
    wanted = row_of_line == jnp.where(inner < MARGIN, leaves, -1000)
    half_matches = second == (lead % (2 * SUB) >= SUB)
    select = jnp.where(wanted & half_matches, 1.0, 0.0).astype(BF16)

    def masks(c):
        column = iota((1, CHUNK), 1) + c * CHUNK
        seen = (column >= columns[0, 0]) & (column < columns[0, 1])
        return jnp.where(seen, 1.0, 0.0).astype(BF16)

    def stacked(block):
        return jnp.concatenate([block[:, :HALF], block[:, HALF:]], axis=0)

    def prepare(c):
        load(c).wait()
        mask = masks(c)
        for p in range(planes):
            block = x[c, p] * mask
            x[c, p] = block
            out = dot(select, stacked(block)).astype(BF16)
            for side in range(SIDES):
                stage[side, c, pl.ds(2 * p * SUB, 2 * SUB), :] = out[
                    side * 2 * SUB : (side + 1) * 2 * SUB
                ]

    prepare(0)

    for copy in small[2:]:
        copy.wait()
    index = iota((1, height), 1)
    valid = (index >= lines[0, 0]) & (index < lines[0, 1])
    weight = jnp.where(valid, blend[...].astype(F32), 0.0)

    k = iota((height, 2 * HALF), 0)
    lane = iota((height, 2 * HALF), 1)
    inner = lane % SUB
    leaves = jnp.where(lane < HALF + HALF // 2, bases[0], bases[1]) + inner
    goes = (lane >= HALF) & (inner < MARGIN) & (k + shift == leaves)
    stays = (lane < HALF) & ((lane == k) | (lane == k + height))
    rows = jnp.broadcast_to(weight, (8, height)).astype(BF16)
    weights = dot(rows, jnp.where(goes | stays, 1.0, 0.0).astype(BF16))
    for side in range(SIDES):
        first = HALF + side * (HALF // 2)
        note[side] = weights[:, first : first + HALF // 2]
    twice = weights[:1, : 2 * height]

    @pl.when(present[1])
    def _():
        pl.semaphore_wait(barrier, 1)
        pl.semaphore_signal(hello, inc=1, device_id={"az": below}, device_id_type=MESH)
        words(1).start()
        outgoing(1, 0).start()

    for c in range(1, chunks):
        prepare(c)

        @pl.when(present[1])
        def _():
            outgoing(1, c).start()

    slot = iota((BLOCK_HEIGHT, 1), 0)
    quad = slot % quads
    second_slot = slot % looks >= quads
    row_in_side = LOOK_ROWS * quad + slot // looks
    keep_f32 = [
        jnp.where(
            (row_of_line == row_in_side + side * quads * LOOK_ROWS) & (second == second_slot),
            twice,
            0.0,
        )
        for side in range(SIDES)
    ]
    keep = jnp.concatenate(keep_f32, axis=0).astype(BF16)

    @pl.when(present[0])
    def _():
        pl.semaphore_wait(hello, 1)
        words(0).start()
        for c in range(chunks):
            outgoing(0, c).start()

    def held(c, carry):
        for p in range(planes):
            out = dot(keep, stacked(x[c, p]))
            for side in range(SIDES):
                own[side, c, p] = out[side * BLOCK_HEIGHT : (side + 1) * BLOCK_HEIGHT]
        return carry

    lax.fori_loop(0, chunks, held, 0)

    def box(c, carry):
        lane = iota((HALF, HALF), 1)
        far = lane >= HALF // 2
        sample = iota((HALF, HALF), 0) + c * CHUNK + jnp.where(far, HALF, 0)
        first = LOOK_COLS * jnp.where(far, lane - HALF // 2, lane)
        inside = (sample >= first) & (sample < first + LOOK_COLS)
        boxes[c] = jnp.where(inside, 1.0, 0.0).astype(BF16)
        return carry

    lax.fori_loop(0, chunks, box, 0)

    def settle(s, carry):
        side = lax.rem(me + s, 2)
        there = (side == 0) & present[0] | (side == 1) & present[1]

        @pl.when(there)
        def _():
            pltpu.make_async_remote_copy(
                src_ref=note.at[side],
                dst_ref=heard.at[side],
                send_sem=note_send.at[side],
                recv_sem=note_recv.at[side],
                device_id={"az": below},
                device_id_type=MESH,
            ).wait_recv()

        lane = iota((1, HALF), 1)
        tile, inner = lane // SUB, lane % SUB
        code = (tile % 2) * 64 + inner + side * LOOK_ROWS
        row_code = jnp.where(second_slot, 64, 0) + row_in_side
        matches = row_code == code
        incoming = jnp.concatenate([heard[side, :1, :]] * 2, axis=1)
        block = jnp.where(matches, incoming, 0.0)
        norm = jnp.sum(jnp.where(tile < 2, block, 0.0), axis=1, keepdims=True)
        stay = jnp.where(side == 0, keep_f32[0], keep_f32[1])
        norm = norm + jnp.sum(stay, axis=1, keepdims=True)
        scale = jnp.broadcast_to(1.0 / norm, (BLOCK_HEIGHT, HALF // 2))
        for p in range(planes):
            spread[pl.ds(p * BLOCK_HEIGHT, BLOCK_HEIGHT), :] = jnp.where(
                tile // 2 == p, block, 0.0
            ).astype(BF16)

        def arrive(c):
            @pl.when(there)
            def _():
                pltpu.make_async_remote_copy(
                    src_ref=stage.at[side, c],
                    dst_ref=recv.at[side, c],
                    send_sem=send_sem.at[side, c],
                    recv_sem=recv_sem.at[side, c],
                    device_id={"az": below},
                    device_id_type=MESH,
                ).wait_recv()

        def spill(c):
            spilled[c % 2] = dot(spread[...], recv[side, c])

        def products(c):
            for b in range(2):
                lanes = pl.ds(b * (HALF // 2), HALF // 2)
                sums = [None] * (images * images)

                def gather(at, value):
                    sums[at] = value if sums[at] is None else sums[at] + value

                for within in range(LOOK_ROWS):
                    own_rows = pl.ds(within * looks, looks)
                    factor = scale[within * looks : (within + 1) * looks]
                    merged = [
                        (
                            spilled[c % 2, pl.ds(p * BLOCK_HEIGHT + within * looks, looks), lanes]
                            + own[side, c, p, own_rows, lanes]
                        )
                        * factor
                        for p in range(planes)
                    ]
                    re, im = merged[:images], merged[images:]
                    for at, (i, j) in enumerate(duos):
                        gather(at, re[i] * re[j] + im[i] * im[j])
                        gather(len(duos) + at, im[i] * re[j] - re[i] * im[j])
                    for i in range(images):
                        gather(2 * len(duos) + i, re[i] * re[i] + im[i] * im[i])
                for at in range(0, images * images, 2):
                    value = jnp.concatenate(sums[at : at + 2], axis=0)
                    high = value.astype(BF16)
                    low = (value - high.astype(F32)).astype(BF16)
                    split[c % 2, 0, pl.ds(at * looks, 2 * looks), lanes] = high
                    split[c % 2, 1, pl.ds(at * looks, 2 * looks), lanes] = low

        def boxed(c):
            part = dot(split[c % 2, 0], boxes[c]) + dot(split[c % 2, 1], boxes[c])
            total[side] = part if c == 0 else total[side] + part

        for c in range(chunks + 2):
            if c < chunks:
                arrive(c)
                spill(c)
            if 1 <= c <= chunks:
                products(c - 1)
            if c >= 2:
                boxed(c - 2)
        return carry

    lax.fori_loop(0, SIDES, settle, 0)

    first_quads = iota((looks, HALF // 2), 0) < quads

    def looked(at):
        rows = pl.ds(at * looks, looks)
        left = [total[side, rows, pl.ds(0, HALF // 2)] for side in range(SIDES)]
        right = [total[side, rows, pl.ds(HALF // 2, HALF // 2)] for side in range(SIDES)]
        return jnp.where(first_quads, left[0] + swap(right[0]), swap(left[1]) + right[1])

    values = [looked(at) for at in range(images * images)]

    def splat(value):
        return jnp.full((looks, HALF // 2), value, I32)

    for p in range(pairs):
        i, j = splat(couples[0, p]), splat(couples[1, p])
        re = im = power_i = power_j = jnp.zeros(i.shape, F32)
        for at, (a, b) in enumerate(duos):
            forward = (i == a) & (j == b)
            backward = (i == b) & (j == a)
            re = jnp.where(forward | backward, values[at], re)
            im = jnp.where(forward, values[len(duos) + at], im)
            im = jnp.where(backward, -values[len(duos) + at], im)
        for a in range(images):
            power_i = jnp.where(i == a, values[2 * len(duos) + a], power_i)
            power_j = jnp.where(j == a, values[2 * len(duos) + a], power_j)
        ifg_ref[0, p] = re / (LOOK_ROWS * LOOK_COLS)
        ifg_ref[1, p] = im / (LOOK_ROWS * LOOK_COLS)
        coh_ref[p] = (re * re + im * im) / jnp.maximum(power_i * power_j, 1.0)

    for side in range(SIDES):

        @pl.when(present[side])
        def _():
            words(side).wait_send()
            for c in range(chunks):
                outgoing(side, c).wait_send()


def write(ifg_ref, coh_ref, ifg_hbm, coh_hbm, sems):
    copies = [
        pltpu.make_async_copy(ifg_ref, ifg_hbm, sems.at[0]),
        pltpu.make_async_copy(coh_ref, coh_hbm, sems.at[1]),
    ]
    for copy in copies:
        copy.start()
    for copy in copies:
        copy.wait()


def per_device(ring, sweep_stack, blend, start, lines, columns, couples):
    parts, images, _, height, width = sweep_stack.shape
    planes = parts * images
    pairs = couples.shape[0]
    chunks = width // CHUNK
    looks = BLOCK_HEIGHT // LOOK_ROWS
    outputs = width // LOOK_COLS
    hbm = pl.BlockSpec(memory_space=pltpu.HBM)
    vmem = pl.BlockSpec(memory_space=pltpu.VMEM)
    ifg_shape, coh_shape = (parts, pairs, looks, outputs), (pairs, looks, outputs)
    ifg, coh = pl.pallas_call(
        functools.partial(merge, ring),
        name="merge",
        out_shape=(pltpu.VMEM(ifg_shape, F32), pltpu.VMEM(coh_shape, F32)),
        in_specs=[hbm] * 6,
        out_specs=(vmem, vmem),
        scratch_shapes=[
            pltpu.VMEM((chunks, planes, height, CHUNK), BF16),
            pltpu.VMEM((SIDES, chunks, planes * 2 * SUB, HALF), BF16),
            pltpu.VMEM((SIDES, chunks, planes * 2 * SUB, HALF), BF16),
            pltpu.VMEM((SIDES, chunks, planes, BLOCK_HEIGHT, HALF), F32),
            pltpu.VMEM((planes * BLOCK_HEIGHT, HALF), BF16),
            pltpu.VMEM((chunks, HALF, HALF), BF16),
            pltpu.VMEM((2, planes * BLOCK_HEIGHT, HALF), F32),
            pltpu.VMEM((2, 2, images * images * looks, HALF), BF16),
            pltpu.VMEM((SIDES, images * images * looks, HALF), F32),
            pltpu.VMEM((SIDES, 8, HALF // 2), F32),
            pltpu.VMEM((SIDES, 8, HALF // 2), F32),
            pltpu.VMEM((1, height), BF16),
            pltpu.SMEM((1, 1), I32),
            pltpu.SMEM((1, 2), I32),
            pltpu.SMEM((1, 2), I32),
            pltpu.SMEM((2, pairs), I32),
            pltpu.SemaphoreType.DMA((chunks,)),
            pltpu.SemaphoreType.DMA((5,)),
            pltpu.SemaphoreType.DMA((SIDES, chunks)),
            pltpu.SemaphoreType.DMA((SIDES, chunks)),
            pltpu.SemaphoreType.DMA((SIDES,)),
            pltpu.SemaphoreType.DMA((SIDES,)),
            pltpu.SemaphoreType.REGULAR,
        ],
        compiler_params=pltpu.CompilerParams(collective_id=0, has_side_effects=True),
    )(
        sweep_stack.reshape(planes, height, width),
        blend,
        start.reshape(1, 1),
        lines,
        columns,
        couples.T,
    )
    return pl.pallas_call(
        write,
        name="write",
        out_shape=(
            jax.ShapeDtypeStruct(ifg_shape, F32),
            jax.ShapeDtypeStruct(coh_shape, F32),
        ),
        in_specs=[vmem, vmem],
        out_specs=(hbm, hbm),
        scratch_shapes=[pltpu.SemaphoreType.DMA((2,))],
        compiler_params=pltpu.CompilerParams(vmem_limit_bytes=1024 * 1024),
    )(ifg, coh)


def solution(mesh):
    return jax.shard_map(
        functools.partial(per_device, mesh.shape["az"]),
        mesh=mesh,
        in_specs=(
            P(None, None, ("groups", "az"), None, None),
            P(("groups", "az"), None),
            P(("groups", "az")),
            P(("groups", "az"), None),
            P(("groups", "az"), None),
            P("groups", None),
        ),
        out_specs=(P(None, "groups", "az", None), P("groups", "az", None)),
        check_vma=False,
    )
```

time: 84.3 us -> 29.3 us (0.35)
  starting transfers between devices: 29.7 us -> 0 us
  Pallas kernels: 0 us -> 27.9 us
  local copies, waits for them, and re-layouts: 25.9 us -> 0 us
  other arithmetic: 22.1 us -> 0 us
  matrix products: 2.61 us -> 0 us
  waiting for transfers between devices: 1.88 us -> 0 us
    ppermute x4 -> x0, starting transfers between devices: 29.7 us -> none  [from_behind(): return lax.ppermute(block, axis, route)]
    pallas_call x0 -> x2, Pallas kernels: none -> 27.9 us  [the longest x1 27.2 us: per_device(): pl.pallas_call(functools.partial(merge, ring), name='merge', out_shape=(p...]
    gather x7 -> x0, local copies, waits for them, and re-layouts: 13.1 us -> none  [the longest x3 7.13 us: gather_lines(): chosen_indices = jnp.take(sweep_content, bounded_indices, axis=2)]
    unnamed x7 -> x0, local copies, waits for them, and re-layouts: 6.1 us -> none
    select_n x8 -> x0, other arithmetic: 5.96 us -> none  [the longest x1 3.01 us: gather_lines(): jnp.where(sample_valid, chosen_indices, jnp.zeros((), jnp.bfloat16))]
    reduce_sum x4 -> x0, other arithmetic: 3.66 us -> none  [the longest x2 3.3 us: looked(): aggregate = jnp.sum(shaped, axis=-2)]
    scatter-add x4 -> x0, other arithmetic: 3.44 us -> none  [the longest x1 1.64 us: per_device(): cross_term = cross_term.at[:, :, :extent_rows].add(from_below)]
    slice x2 -> x0, local copies, waits for them, and re-layouts: 2.69 us -> none  [the longest x1 1.38 us: per_device(): usable_azimuth_extent[0, 0]]
  transfers between devices with their start and end apart: 4 -> 0, of which waited for: 1 -> 0; matrix products, arithmetic and copies ran while one was open for 26% -> 0% of each run, Pallas kernels for 0% -> 0%
where the time goes in v2:
time: 29.3 us; the launch traced here: 29.2 us
  Pallas kernels  27.9 us (95%)
  between operations  1.28 us (4%)
    pallas_call x1, Pallas kernels, per_device(): pl.pallas_call(functools.partial(merge, ring), name='merge', out_shape=(p...  27.2 us
    pallas_call x1, Pallas kernels, per_device(): pl.pallas_call(write, name='write', out_shape=(jax.ShapeDtypeStruct(ifg_s...  0.64 us

profile of v2, /device:TPU:37, one launch (start us, length us, event | category | flops | bytes accessed | tf_op | source)
XLA Modules:
  0.0 29.2 jit_solution(1620968892572475506)
XLA Ops:
  1.3 27.2 %merge.1 = (f32[2,4,8,128]{3,2,1,0:T(8,128)S(1)}, f32[4,8,128]{2,1,0:T(8,128)S(1)}) custom-call(bf16[8,80,2560]{2,1,0:T(8,128)(2,1)} %bitcast.4, bf16[1,80]{1,0:T(2,128)(2,1)} %blend_hbm.1, s32[1,1]{1,0:T(1,128)} %bitcast.3.start_hbm, s32[1,2]{1,0:T(1,128)} %lines_hbm.1, s32[1,2]{1,0:T(1,128)} %columns_hbm.1, s32[2,4]{1,0:T(2,128)} %bitcast.5), custom_call_target="tpu_custom_call" | custom-call | tf_op jit(solution)/shard_map/merge/pallas_call | solution.py:406
  28.5 0.6 %write.1 = (f32[2,4,8,128]{3,2,1,0:T(8,128)}, f32[4,8,128]{2,1,0:T(8,128)}) custom-call(f32[2,4,8,128]{3,2,1,0:T(8,128)S(1)} %get-tuple-element.4.ifg_ref, f32[4,8,128]{2,1,0:T(8,128)S(1)} %get-tuple-element.5.coh_ref), custom_call_target="tpu_custom_call" | custom-call | tf_op jit(solution)/shard_map/write/pallas_call | solution.py:446

commit v3 on v2

--- a/solution.py
+++ b/solution.py
@@ -174,8 +174,6 @@
                     side * 2 * SUB : (side + 1) * 2 * SUB
                 ]
 
-    prepare(0)
-
     for copy in small[2:]:
         copy.wait()
     index = iota((1, height), 1)
@@ -200,14 +198,25 @@
         pl.semaphore_wait(barrier, 1)
         pl.semaphore_signal(hello, inc=1, device_id={"az": below}, device_id_type=MESH)
         words(1).start()
-        outgoing(1, 0).start()
-
-    for c in range(1, chunks):
+
+    for c in range(chunks):
         prepare(c)
 
         @pl.when(present[1])
         def _():
             outgoing(1, c).start()
+
+    def send_up():
+        pl.semaphore_wait(hello, 1)
+        words(0).start()
+        for c in range(chunks):
+            outgoing(0, c).start()
+
+    linked = me % 2 == 0
+
+    @pl.when(present[0] & linked)
+    def _():
+        send_up()
 
     slot = iota((BLOCK_HEIGHT, 1), 0)
     quad = slot % quads
@@ -223,13 +232,6 @@
     ]
     keep = jnp.concatenate(keep_f32, axis=0).astype(BF16)
 
-    @pl.when(present[0])
-    def _():
-        pl.semaphore_wait(hello, 1)
-        words(0).start()
-        for c in range(chunks):
-            outgoing(0, c).start()
-
     def held(c, carry):
         for p in range(planes):
             out = dot(keep, stacked(x[c, p]))
@@ -253,6 +255,10 @@
     def settle(s, carry):
         side = lax.rem(me + s, 2)
         there = (side == 0) & present[0] | (side == 1) & present[1]
+
+        @pl.when((s == 1) & present[0] & jnp.logical_not(linked))
+        def _():
+            send_up()
 
         @pl.when(there)
         def _():

time: 29.3 us -> 27.1 us (0.925)
  Pallas kernels: 27.9 us -> 25.7 us
    pallas_call x1, Pallas kernels: 27.2 us -> 25.1 us  [per_device(): pl.pallas_call(functools.partial(merge, ring), name='merge', out_shape=(p...]
where the time goes in v3:
time: 27.1 us; the launch traced here: 27 us
  Pallas kernels  25.7 us (95%)
  between operations  1.28 us (5%)
    pallas_call x1, Pallas kernels, per_device(): pl.pallas_call(functools.partial(merge, ring), name='merge', out_shape=(p...  25.1 us
    pallas_call x1, Pallas kernels, per_device(): pl.pallas_call(write, name='write', out_shape=(jax.ShapeDtypeStruct(ifg_s...  0.64 us

profile of v3, /device:TPU:37, one launch (start us, length us, event | category | flops | bytes accessed | tf_op | source)
XLA Modules:
  0.0 27.0 jit_solution(18065375956075060728)
XLA Ops:
  1.3 25.1 %merge.1 = (f32[2,4,8,128]{3,2,1,0:T(8,128)S(1)}, f32[4,8,128]{2,1,0:T(8,128)S(1)}) custom-call(bf16[8,80,2560]{2,1,0:T(8,128)(2,1)} %bitcast.4, bf16[1,80]{1,0:T(2,128)(2,1)} %blend_hbm.1, s32[1,1]{1,0:T(1,128)} %bitcast.3.start_hbm, s32[1,2]{1,0:T(1,128)} %lines_hbm.1, s32[1,2]{1,0:T(1,128)} %columns_hbm.1, s32[2,4]{1,0:T(2,128)} %bitcast.5), custom_call_target="tpu_custom_call" | custom-call | tf_op jit(solution)/shard_map/merge/pallas_call | solution.py:412
  26.4 0.6 %write.1 = (f32[2,4,8,128]{3,2,1,0:T(8,128)}, f32[4,8,128]{2,1,0:T(8,128)}) custom-call(f32[2,4,8,128]{3,2,1,0:T(8,128)S(1)} %get-tuple-element.4.ifg_ref, f32[4,8,128]{2,1,0:T(8,128)S(1)} %get-tuple-element.5.coh_ref), custom_call_target="tpu_custom_call" | custom-call | tf_op jit(solution)/shard_map/write/pallas_call | solution.py:452

commit v4 on v3

--- a/solution.py
+++ b/solution.py
@@ -13,7 +13,7 @@
 MARGIN = 15
 HALF = 256
 CHUNK = 2 * HALF
-SUB = 16
+SPILL_ROWS = 32
 SIDES = 2
 F32, BF16, I32 = jnp.float32, jnp.bfloat16, jnp.int32
 MESH = pl.DeviceIdType.MESH
@@ -46,10 +46,9 @@
     stage,
     recv,
     own,
-    spread,
     boxes,
-    spilled,
     split,
+    norms,
     total,
     note,
     heard,
@@ -95,19 +94,17 @@
             x_hbm.at[:, :, pl.ds(c * CHUNK, CHUNK)], x.at[c], x_sem.at[c]
         )
 
-    for copy in small[:3]:
+    for copy in small:
         copy.start()
     load(0).start()
-    for copy in small[3:]:
-        copy.start()
-    for c in range(1, chunks):
-        load(c).start()
-
     barrier = pltpu.get_barrier_semaphore()
 
     @pl.when(present[0])
     def _():
         pl.semaphore_signal(barrier, inc=1, device_id={"az": above}, device_id_type=MESH)
+
+    for c in range(1, chunks):
+        load(c).start()
 
     for side in range(SIDES):
 
@@ -137,7 +134,12 @@
             device_id_type=MESH,
         )
 
-    for copy in small[:2]:
+    @pl.when(present[1])
+    def _():
+        pl.semaphore_wait(barrier, 1)
+        pl.semaphore_signal(hello, inc=1, device_id={"az": below}, device_id_type=MESH)
+
+    for copy in small[:4]:
         copy.wait()
     shift = start[0, 0] - me * BLOCK_HEIGHT
     bases = (-MARGIN, BLOCK_HEIGHT)
@@ -147,12 +149,14 @@
     line = jnp.where(second, place - height, place)
     row_of_line = line + shift
 
-    lead = iota((SIDES * 2 * SUB, 1), 0)
-    inner = lead % SUB
-    leaves = jnp.where(lead < 2 * SUB, bases[0], bases[1]) + inner
-    wanted = row_of_line == jnp.where(inner < MARGIN, leaves, -1000)
-    half_matches = second == (lead % (2 * SUB) >= SUB)
-    select = jnp.where(wanted & half_matches, 1.0, 0.0).astype(BF16)
+    def travels(rows):
+        quad, register = rows % quads, rows // looks % quads
+        row = jnp.where(quad < quads - 1, LOOK_ROWS * quad + register, LOOK_ROWS * (register + 1) - 1)
+        return jnp.where((quad == quads - 1) & (register == quads - 1), -1000, row)
+
+    lead = iota((SIDES * SPILL_ROWS, 1), 0)
+    wanted = row_of_line == travels(lead) + jnp.where(lead < SPILL_ROWS, bases[0], bases[1])
+    select = jnp.where(wanted & (second == (lead % looks >= quads)), 1.0, 0.0).astype(BF16)
 
     def masks(c):
         column = iota((1, CHUNK), 1) + c * CHUNK
@@ -162,48 +166,45 @@
     def stacked(block):
         return jnp.concatenate([block[:, :HALF], block[:, HALF:]], axis=0)
 
+    high_half = iota((SPILL_ROWS // 2, HALF), 0) % looks >= quads
+
     def prepare(c):
         load(c).wait()
-        mask = masks(c)
+        if c == 0:
+            describe()
+        mask = masks(c).astype(F32)
+        mask = jnp.where(
+            high_half,
+            jnp.broadcast_to(mask[:, HALF:], high_half.shape),
+            jnp.broadcast_to(mask[:, :HALF], high_half.shape),
+        ).astype(BF16)
+        mask = jnp.concatenate([mask] * (2 * SIDES), axis=0)
         for p in range(planes):
-            block = x[c, p] * mask
-            x[c, p] = block
-            out = dot(select, stacked(block)).astype(BF16)
+            out = dot(select, stacked(x[c, p])).astype(BF16) * mask
             for side in range(SIDES):
-                stage[side, c, pl.ds(2 * p * SUB, 2 * SUB), :] = out[
-                    side * 2 * SUB : (side + 1) * 2 * SUB
-                ]
-
-    for copy in small[2:]:
-        copy.wait()
+                stage[side, c, p] = out[side * SPILL_ROWS : (side + 1) * SPILL_ROWS]
+
     index = iota((1, height), 1)
     valid = (index >= lines[0, 0]) & (index < lines[0, 1])
     weight = jnp.where(valid, blend[...].astype(F32), 0.0)
 
-    k = iota((height, 2 * HALF), 0)
-    lane = iota((height, 2 * HALF), 1)
-    inner = lane % SUB
-    leaves = jnp.where(lane < HALF + HALF // 2, bases[0], bases[1]) + inner
-    goes = (lane >= HALF) & (inner < MARGIN) & (k + shift == leaves)
-    stays = (lane < HALF) & ((lane == k) | (lane == k + height))
-    rows = jnp.broadcast_to(weight, (8, height)).astype(BF16)
-    weights = dot(rows, jnp.where(goes | stays, 1.0, 0.0).astype(BF16))
-    for side in range(SIDES):
-        first = HALF + side * (HALF // 2)
-        note[side] = weights[:, first : first + HALF // 2]
-    twice = weights[:1, : 2 * height]
-
-    @pl.when(present[1])
-    def _():
-        pl.semaphore_wait(barrier, 1)
-        pl.semaphore_signal(hello, inc=1, device_id={"az": below}, device_id_type=MESH)
-        words(1).start()
+    slot = iota((BLOCK_HEIGHT, 1), 0)
+    quad, within_look = slot % quads, slot // looks
+    second_slot = slot % looks >= quads
+
+    def describe():
+        for side in range(SIDES):
+            goes = jnp.where(quad < quads - 1, LOOK_ROWS * quad + within_look + bases[side], -1000)
+            sent = jnp.where(index + shift == goes, weight, 0.0)
+            note[side] = jnp.broadcast_to(jnp.sum(sent, axis=1, keepdims=True), note.shape[1:])
 
     for c in range(chunks):
         prepare(c)
 
         @pl.when(present[1])
         def _():
+            if c == 0:
+                words(1).start()
             outgoing(1, c).start()
 
     def send_up():
@@ -218,23 +219,26 @@
     def _():
         send_up()
 
-    slot = iota((BLOCK_HEIGHT, 1), 0)
-    quad = slot % quads
-    second_slot = slot % looks >= quads
-    row_in_side = LOOK_ROWS * quad + slot // looks
-    keep_f32 = [
-        jnp.where(
-            (row_of_line == row_in_side + side * quads * LOOK_ROWS) & (second == second_slot),
-            twice,
-            0.0,
-        )
-        for side in range(SIDES)
-    ]
-    keep = jnp.concatenate(keep_f32, axis=0).astype(BF16)
+    k = iota((height, HALF), 0)
+    lane = iota((height, HALF), 1)
+    copies = jnp.where((lane == k) | (lane == k + height), 1.0, 0.0).astype(BF16)
+    rows = jnp.broadcast_to(weight, (8, height)).astype(BF16)
+    twice = dot(rows, copies)[:1, : 2 * height]
+
+    keep = []
+    for side in range(SIDES):
+        look = quad if side == 0 else quads + (quad + 1) % quads
+        stays = (row_of_line == LOOK_ROWS * look + within_look) & (second == second_slot)
+        keep.append(jnp.where(stays, twice, 0.0))
+        norms[side] = jnp.broadcast_to(
+            jnp.sum(keep[side], axis=1, keepdims=True), norms.shape[1:]
+        )
+    keep = jnp.concatenate(keep, axis=0).astype(BF16)
 
     def held(c, carry):
+        mask = masks(c)
         for p in range(planes):
-            out = dot(keep, stacked(x[c, p]))
+            out = dot(keep, stacked(x[c, p] * mask))
             for side in range(SIDES):
                 own[side, c, p] = out[side * BLOCK_HEIGHT : (side + 1) * BLOCK_HEIGHT]
         return carry
@@ -271,21 +275,18 @@
                 device_id_type=MESH,
             ).wait_recv()
 
-        lane = iota((1, HALF), 1)
-        tile, inner = lane // SUB, lane % SUB
-        code = (tile % 2) * 64 + inner + side * LOOK_ROWS
-        row_code = jnp.where(second_slot, 64, 0) + row_in_side
-        matches = row_code == code
-        incoming = jnp.concatenate([heard[side, :1, :]] * 2, axis=1)
-        block = jnp.where(matches, incoming, 0.0)
-        norm = jnp.sum(jnp.where(tile < 2, block, 0.0), axis=1, keepdims=True)
-        stay = jnp.where(side == 0, keep_f32[0], keep_f32[1])
-        norm = norm + jnp.sum(stay, axis=1, keepdims=True)
-        scale = jnp.broadcast_to(1.0 / norm, (BLOCK_HEIGHT, HALF // 2))
-        for p in range(planes):
-            spread[pl.ds(p * BLOCK_HEIGHT, BLOCK_HEIGHT), :] = jnp.where(
-                tile // 2 == p, block, 0.0
-            ).astype(BF16)
+        scale = 1.0 / (norms[side] + heard[side])
+        factor = heard[side] * scale
+
+        def rescale(c, carry):
+            for p in range(planes):
+                for b in range(2):
+                    lanes = pl.ds(b * (HALF // 2), HALF // 2)
+                    own[side, c, p, :, lanes] = own[side, c, p, :, lanes] * scale
+            return carry
+
+        lax.fori_loop(0, chunks, rescale, 0)
+        third = iota((looks, HALF // 2), 0) % quads
 
         def arrive(c):
             @pl.when(there)
@@ -299,9 +300,6 @@
                     device_id_type=MESH,
                 ).wait_recv()
 
-        def spill(c):
-            spilled[c % 2] = dot(spread[...], recv[side, c])
-
         def products(c):
             for b in range(2):
                 lanes = pl.ds(b * (HALF // 2), HALF // 2)
@@ -310,15 +308,23 @@
                 def gather(at, value):
                     sums[at] = value if sums[at] is None else sums[at] + value
 
+                spills = []
+                for p in range(planes):
+                    block = recv[side, c, p, :, lanes].astype(F32)
+                    parts = [block[v * looks : (v + 1) * looks] for v in range(quads)]
+                    turned = [
+                        pltpu.roll(parts[v], looks - (quads - 1) + v, 0) for v in range(quads - 1)
+                    ]
+                    last = turned[quads - 2]
+                    for v in range(quads - 2):
+                        last = jnp.where(third == v, turned[v], last)
+                    spills.append(parts + [last])
+
                 for within in range(LOOK_ROWS):
-                    own_rows = pl.ds(within * looks, looks)
-                    factor = scale[within * looks : (within + 1) * looks]
+                    rows = pl.ds(within * looks, looks)
+                    weights = factor[within * looks : (within + 1) * looks]
                     merged = [
-                        (
-                            spilled[c % 2, pl.ds(p * BLOCK_HEIGHT + within * looks, looks), lanes]
-                            + own[side, c, p, own_rows, lanes]
-                        )
-                        * factor
+                        own[side, c, p, rows, lanes] + spills[p][within] * weights
                         for p in range(planes)
                     ]
                     re, im = merged[:images], merged[images:]
@@ -338,25 +344,28 @@
             part = dot(split[c % 2, 0], boxes[c]) + dot(split[c % 2, 1], boxes[c])
             total[side] = part if c == 0 else total[side] + part
 
-        for c in range(chunks + 2):
+        for c in range(chunks + 1):
             if c < chunks:
                 arrive(c)
-                spill(c)
-            if 1 <= c <= chunks:
-                products(c - 1)
-            if c >= 2:
-                boxed(c - 2)
+                products(c)
+            if c >= 1:
+                boxed(c - 1)
         return carry
 
     lax.fori_loop(0, SIDES, settle, 0)
 
-    first_quads = iota((looks, HALF // 2), 0) < quads
+    small[4].wait()
+    sublane = iota((looks, HALF // 2), 0)
 
     def looked(at):
         rows = pl.ds(at * looks, looks)
         left = [total[side, rows, pl.ds(0, HALF // 2)] for side in range(SIDES)]
         right = [total[side, rows, pl.ds(HALF // 2, HALF // 2)] for side in range(SIDES)]
-        return jnp.where(first_quads, left[0] + swap(right[0]), swap(left[1]) + right[1])
+        top, bottom = [left[side] + swap(right[side]) for side in range(SIDES)]
+        bottom = jnp.where(
+            sublane == quads, pltpu.roll(bottom, 1, 0), pltpu.roll(bottom, quads + 1, 0)
+        )
+        return jnp.where(sublane < quads, top, bottom)
 
     values = [looked(at) for at in range(images * images)]
 
@@ -417,16 +426,15 @@
         out_specs=(vmem, vmem),
         scratch_shapes=[
             pltpu.VMEM((chunks, planes, height, CHUNK), BF16),
-            pltpu.VMEM((SIDES, chunks, planes * 2 * SUB, HALF), BF16),
-            pltpu.VMEM((SIDES, chunks, planes * 2 * SUB, HALF), BF16),
+            pltpu.VMEM((SIDES, chunks, planes, SPILL_ROWS, HALF), BF16),
+            pltpu.VMEM((SIDES, chunks, planes, SPILL_ROWS, HALF), BF16),
             pltpu.VMEM((SIDES, chunks, planes, BLOCK_HEIGHT, HALF), F32),
-            pltpu.VMEM((planes * BLOCK_HEIGHT, HALF), BF16),
             pltpu.VMEM((chunks, HALF, HALF), BF16),
-            pltpu.VMEM((2, planes * BLOCK_HEIGHT, HALF), F32),
             pltpu.VMEM((2, 2, images * images * looks, HALF), BF16),
+            pltpu.VMEM((SIDES, BLOCK_HEIGHT, HALF // 2), F32),
             pltpu.VMEM((SIDES, images * images * looks, HALF), F32),
-            pltpu.VMEM((SIDES, 8, HALF // 2), F32),
-            pltpu.VMEM((SIDES, 8, HALF // 2), F32),
+            pltpu.VMEM((SIDES, BLOCK_HEIGHT, HALF // 2), F32),
+            pltpu.VMEM((SIDES, BLOCK_HEIGHT, HALF // 2), F32),
             pltpu.VMEM((1, height), BF16),
             pltpu.SMEM((1, 1), I32),
             pltpu.SMEM((1, 2), I32),

time: 27.1 us -> 26.6 us (0.982)
  Pallas kernels: 25.7 us -> 25.2 us
    pallas_call x1, Pallas kernels: 25.1 us -> 24.6 us  [per_device(): pl.pallas_call(functools.partial(merge, ring), name='merge', out_shape=(p...]
where the time goes in v4:
time: 26.6 us; the launch traced here: 26.5 us
  Pallas kernels  25.2 us (95%)
  between operations  1.28 us (5%)
    pallas_call x1, Pallas kernels, per_device(): pl.pallas_call(functools.partial(merge, ring), name='merge', out_shape=(p...  24.6 us
    pallas_call x1, Pallas kernels, per_device(): pl.pallas_call(write, name='write', out_shape=(jax.ShapeDtypeStruct(ifg_s...  0.64 us

profile of v4, /device:TPU:37, one launch (start us, length us, event | category | flops | bytes accessed | tf_op | source)
XLA Modules:
  0.0 26.5 jit_solution(10249320625457569757)
XLA Ops:
  1.3 24.6 %merge.1 = (f32[2,4,8,128]{3,2,1,0:T(8,128)S(1)}, f32[4,8,128]{2,1,0:T(8,128)S(1)}) custom-call(bf16[8,80,2560]{2,1,0:T(8,128)(2,1)} %bitcast.4, bf16[1,80]{1,0:T(2,128)(2,1)} %blend_hbm.1, s32[1,1]{1,0:T(1,128)} %bitcast.3.start_hbm, s32[1,2]{1,0:T(1,128)} %lines_hbm.1, s32[1,2]{1,0:T(1,128)} %columns_hbm.1, s32[2,4]{1,0:T(2,128)} %bitcast.5), custom_call_target="tpu_custom_call" | custom-call | tf_op jit(solution)/shard_map/merge/pallas_call | solution.py:421
  25.9 0.6 %write.1 = (f32[2,4,8,128]{3,2,1,0:T(8,128)}, f32[4,8,128]{2,1,0:T(8,128)}) custom-call(f32[2,4,8,128]{3,2,1,0:T(8,128)S(1)} %get-tuple-element.4.ifg_ref, f32[4,8,128]{2,1,0:T(8,128)S(1)} %get-tuple-element.5.coh_ref), custom_call_target="tpu_custom_call" | custom-call | tf_op jit(solution)/shard_map/write/pallas_call | solution.py:460

commit v5 on v4

--- a/solution.py
+++ b/solution.py
@@ -198,6 +198,12 @@
             sent = jnp.where(index + shift == goes, weight, 0.0)
             note[side] = jnp.broadcast_to(jnp.sum(sent, axis=1, keepdims=True), note.shape[1:])
 
+    linked = me % 2 == 0
+
+    def greet():
+        pl.semaphore_wait(hello, 1)
+        words(0).start()
+
     for c in range(chunks):
         prepare(c)
 
@@ -207,17 +213,19 @@
                 words(1).start()
             outgoing(1, c).start()
 
-    def send_up():
-        pl.semaphore_wait(hello, 1)
-        words(0).start()
-        for c in range(chunks):
-            outgoing(0, c).start()
-
-    linked = me % 2 == 0
-
-    @pl.when(present[0] & linked)
-    def _():
-        send_up()
+        if c == 1:
+
+            @pl.when(present[0] & linked)
+            def _():
+                greet()
+                for earlier in range(c + 1):
+                    outgoing(0, earlier).start()
+
+        elif c > 1:
+
+            @pl.when(present[0] & linked)
+            def _():
+                outgoing(0, c).start()
 
     k = iota((height, HALF), 0)
     lane = iota((height, HALF), 1)
@@ -256,13 +264,15 @@
 
     lax.fori_loop(0, chunks, box, 0)
 
+    @pl.when(present[0] & jnp.logical_not(linked))
+    def _():
+        greet()
+        for c in range(chunks):
+            outgoing(0, c).start()
+
     def settle(s, carry):
         side = lax.rem(me + s, 2)
         there = (side == 0) & present[0] | (side == 1) & present[1]
-
-        @pl.when((s == 1) & present[0] & jnp.logical_not(linked))
-        def _():
-            send_up()
 
         @pl.when(there)
         def _():

time: 26.6 us -> 26.6 us (level)
  no operation moved by 1% of the time
where the time goes in v5:
time: 26.6 us; the launch traced here: 26.5 us
  Pallas kernels  25.2 us (95%)
  between operations  1.28 us (5%)
    pallas_call x1, Pallas kernels, per_device(): pl.pallas_call(functools.partial(merge, ring), name='merge', out_shape=(p...  24.6 us
    pallas_call x1, Pallas kernels, per_device(): pl.pallas_call(write, name='write', out_shape=(jax.ShapeDtypeStruct(ifg_s...  0.64 us

profile of v5, /device:TPU:37, one launch (start us, length us, event | category | flops | bytes accessed | tf_op | source)
XLA Modules:
  0.0 26.5 jit_solution(11800573379332350500)
XLA Ops:
  1.3 24.6 %merge.1 = (f32[2,4,8,128]{3,2,1,0:T(8,128)S(1)}, f32[4,8,128]{2,1,0:T(8,128)S(1)}) custom-call(bf16[8,80,2560]{2,1,0:T(8,128)(2,1)} %bitcast.4, bf16[1,80]{1,0:T(2,128)(2,1)} %blend_hbm.1, s32[1,1]{1,0:T(1,128)} %bitcast.3.start_hbm, s32[1,2]{1,0:T(1,128)} %lines_hbm.1, s32[1,2]{1,0:T(1,128)} %columns_hbm.1, s32[2,4]{1,0:T(2,128)} %bitcast.5), custom_call_target="tpu_custom_call" | custom-call | tf_op jit(solution)/shard_map/merge/pallas_call | solution.py:431
  25.9 0.6 %write.1 = (f32[2,4,8,128]{3,2,1,0:T(8,128)}, f32[4,8,128]{2,1,0:T(8,128)}) custom-call(f32[2,4,8,128]{3,2,1,0:T(8,128)S(1)} %get-tuple-element.4.ifg_ref, f32[4,8,128]{2,1,0:T(8,128)S(1)} %get-tuple-element.5.coh_ref), custom_call_target="tpu_custom_call" | custom-call | tf_op jit(solution)/shard_map/write/pallas_call | solution.py:470
